TPU v7x, 256 devices: a whole 4x4x8 slice. The times are simulated.
256 devices in a mesh: seq: 64 (over z, x, core), head: 4 (over y).
Axes of the slice: x: 4, y: 4, z: 8, core: 2. Of those that a mesh axis runs over, the one named last changes fastest.
Arguments:
- tokens: bfloat16 [65536, 2048], P('seq', 'head'), may hold values from -8 to 8
- w_query: bfloat16 [2048, 2048], P(None, 'head'), may hold values from -1 to 1, as said below
- w_key: bfloat16 [2048, 2048], P(None, 'head'), may hold values from -1 to 1, as said below
- w_value: bfloat16 [2048, 2048], P(None, 'head'), may hold values from -0.125 to 0.125
- w_out: bfloat16 [2048, 2048], P('head'), may hold values from -0.125 to 0.125
- mix_logit: float32 [8], P('head'), may hold values from -2 to 2
Outputs:
- layer_out: bfloat16 [65536, 2048], P('seq', 'head')
Inputs may be any that keep to these rules, and one draw needn't show every extreme that they name: `w_query`: entries of mean zero with a standard deviation of about 2048 ** -0.5. `w_key`: entries of mean zero with a standard deviation of about 2048 ** -0.5.
All inputs are finite; a program needn't handle non-finite values.
Results may differ from a plain program's by a relative error of at most 0.0065.
Values may be sent and summed in bfloat16 or wider, within the bound.
A program may use at most 128 MiB of HBM per device.

v0:
```python
import jax
import jax.numpy as jnp
from jax import lax
from jax.sharding import Mesh
from jax.sharding import PartitionSpec as P

SEQ = ("seq_0", "seq_1", "seq_2")


def nothing_yet(shard, identity):
    return jax.tree.map(
        lambda a, e: jnp.broadcast_to(jnp.asarray(e, a.dtype), a.shape), shard, identity
    )


def carried_in(shard, axes, combine, identity):
    before = start = nothing_yet(shard, identity)
    running = shard
    for axis in reversed(axes):
        length, mine = (lax.axis_size(axis), lax.axis_index(axis))
        pieces = jax.tree.map(
            lambda part, kind: lax.all_gather(part.astype(kind), axis),
            running,
            (jnp.bfloat16, jnp.bfloat16),
        )
        inside, running = (start, start)
        for k in range(length):
            passed = k < mine
            running = combine(
                running, jax.tree.map(lambda part, own: part[k].astype(own.dtype), pieces, shard)
            )
            inside = jax.tree.map(lambda new, old: jnp.where(passed, new, old), running, inside)
        before = combine(inside, before)
    return before


def feature(values):
    return jax.nn.elu(values) + 1.0


def add_pairs(earlier, later):
    return (earlier[0] + later[0], earlier[1] + later[1])


def on_device(tokens, w_query, w_key, w_value, w_out, mix_logit):
    seg = tokens.shape[0]
    heads = mix_logit.shape[0]
    width = w_query.shape[1]
    hsize = width // heads
    empty = jnp.zeros((seg, width), jnp.float32)
    totals = (empty, empty, empty)
    piece = lax.all_gather(tokens, "head", axis=1, tiled=True)
    result = []
    for total, weight in zip(totals, (w_query, w_key, w_value)):
        result.append(jnp.dot(piece, weight, preferred_element_type=jnp.float32))
    query, keys, values = tuple(result)
    query = query.astype(jnp.bfloat16).reshape(seg, heads, hsize)
    keys = keys.astype(jnp.bfloat16).reshape(seg, heads, hsize)
    values = values.astype(jnp.bfloat16).reshape(seg, heads, hsize)
    fkey = feature(keys.astype(jnp.float32)).astype(jnp.bfloat16)
    mem_term = jnp.einsum("thd,the->hde", fkey, values, preferred_element_type=jnp.float32)
    norm_term = jnp.sum(fkey.astype(jnp.float32), axis=0)
    zeros_pair = (jnp.zeros_like(mem_term), jnp.zeros_like(norm_term))
    memory, normal = carried_in((mem_term, norm_term), SEQ, add_pairs, zeros_pair)
    rows = lax.broadcasted_iota(jnp.int32, (seg, seg), 0)
    cols = lax.broadcasted_iota(jnp.int32, (seg, seg), 1)
    causal = cols <= rows
    scale = 1.0 / hsize**0.5
    scores = jnp.einsum("qhd,khd->hqk", query, keys, preferred_element_type=jnp.float32) * scale
    scores = jnp.where(causal[None], scores, -1e30)
    expo = jnp.exp(scores - jnp.max(scores, axis=2, keepdims=True))
    probs = (expo / jnp.sum(expo, axis=2, keepdims=True)).astype(jnp.bfloat16)
    local = jnp.einsum("hqk,khd->qhd", probs, values, preferred_element_type=jnp.float32)
    fquery = feature(query.astype(jnp.float32)).astype(jnp.bfloat16).astype(jnp.float32)
    numer = jnp.einsum("thd,hde->the", fquery, memory, precision=lax.Precision.HIGHEST)
    denom = jnp.einsum("thd,hd->th", fquery, normal, precision=lax.Precision.HIGHEST)
    readout = numer / jnp.maximum(denom, 1.0)[:, :, None]
    share = jax.nn.sigmoid(mix_logit)[None, :, None]
    mixed = (share * readout + (1.0 - share) * local).astype(jnp.bfloat16).reshape(seg, width)
    columns = lax.all_to_all(w_out, "head", split_axis=1, concat_axis=0, tiled=True)
    summed = jnp.dot(
        lax.all_gather(mixed, "head", axis=1, tiled=True),
        columns,
        preferred_element_type=jnp.float32,
    )
    return summed.astype(jnp.bfloat16)


def solution(mesh):
    torus = Mesh(
        mesh.devices.reshape(8, 4, 2, mesh.shape["head"]), ("seq_0", "seq_1", "seq_2", "head")
    )
    return jax.shard_map(
        on_device,
        mesh=torus,
        in_specs=(
            P(SEQ, "head"),
            P(None, "head"),
            P(None, "head"),
            P(None, "head"),
            P("head", None),
            P("head"),
        ),
        out_specs=P(SEQ, "head"),
        check_vma=False,
    )
```

profile of v0, /device:TPU:1, one launch (start us, length us, event | category | flops | bytes accessed | tf_op | source)
XLA Modules:
  0.0 251.1 jit_solution(9462103053753191697)
XLA Ops:
  6.5 0.0 copy-start
  6.5 0.0 all-gather.6.cloned.1.call-start
  6.5 0.7 all-gather.6.cloned.1.call-update
  7.3 0.0 all-gather.8.cloned.1.call-start
  7.3 56.3 %all-gather.6.cloned.1.call-done = bf16[1024,2048]{1,0:T(8,128)(2,1)} async-done(((bf16[1024,512]{1,0:T(8,128)(2,1)}), bf16[1024,2048]{1,0:T(8,128)(2,1)}) %all-gather.6.cloned.1.call-update) | async-done | bytes 4194320 | tf_op jit(solution)/shard_map/all_gather | solution.py:52
  63.6 0.0 copy-done
  63.6 6.2 %fusion.20 = (bf16[512]{0:T(512)(128)(2,1)S(1)}, bf16[1024,512]{0,1:T(8,128)(2,1)}) fusion(bf16[1024,2048]{1,0:T(8,128)(2,1)} %all-gather.6.cloned.1.call-done, bf16[2048,512]{1,0:T(8,128)(2,1)S(1)} %copy-done), kind=kOutput, calls=%fused_computation.36 | convolution fusion | flops 2151677440 | bytes 7341056 | tf_op jit(solution)/shard_map/dot_general | solution.py:55
  69.8 2.3 copy.33
  72.1 0.0 copy-start.1
  72.1 5.3 %convolution_convert_fusion.2 = bf16[1024,512]{0,1:T(8,128)(2,1)S(1)} fusion(bf16[1024,2048]{1,0:T(8,128)(2,1)} %all-gather.6.cloned.1.call-done, bf16[2048,512]{1,0:T(8,128)(2,1)} %param.9), kind=kOutput, calls=%fused_computation.31 | convolution fusion | flops 2148007936 | bytes 7340032 | tf_op jit(solution)/shard_map/dot_general | solution.py:55
  77.4 0.0 copy-start.3
  77.4 0.0 copy-done.1
  77.4 0.0 copy-start.2
  77.4 1.2 convolution_convert_fusion.4
  78.7 0.0 copy-done.3
  78.7 2.7 %all-gather = bf16[4,256,256]{2,1,0:T(8,128)(2,1)S(1)} all-gather(bf16[2,256,256]{2,1,0:T(8,128)(2,1)S(1)} %convolution_convert_fusion.4), channel_id=2, replica_groups=mesh['seq_0'=8,'seq_1'=4,'seq_2'=2,'head'=4] {'seq_2'}, dimensions={0}, use_global_device_ids=true | all-gather | bytes 786432 | tf_op jit(solution)/shard_map/all_gather | solution.py:22
  81.3 0.8 fusion.59
  82.1 0.0 all-gather.8.cloned.1.call-update
  82.1 0.0 all-gather.10.cloned.1.call-start
  82.2 0.0 copy-done.2
  82.2 24.7 %all-gather.8.cloned.1.call-done = bf16[4,2,256,256]{3,2,1,0:T(8,128)(2,1)} async-done(((bf16[1,2,256,256]{3,2,1,0:T(8,128)(2,1)}), bf16[4,2,256,256]{3,2,1,0:T(8,128)(2,1)}) %all-gather.8.cloned.1.call-update) | async-done | bytes 1048592 | tf_op jit(solution)/shard_map/all_gather | solution.py:22
  106.9 2.0 fusion.55
  108.9 0.0 all-gather.10.cloned.1.call-update
  108.9 0.0 all-gather.12.cloned.1.call-start
  109.0 1.3 iota_compare_fusion
  110.3 6.2 %convolution_convert_fusion.1 = bf16[1024,512]{0,1:T(8,128)(2,1)} fusion(bf16[1024,2048]{1,0:T(8,128)(2,1)} %all-gather.6.cloned.1.call-done, bf16[2048,512]{1,0:T(8,128)(2,1)} %param.7), kind=kOutput, calls=%fused_computation.30 | convolution fusion | flops 2148007936 | bytes 7340032 | tf_op jit(solution)/shard_map/dot_general | solution.py:55
  116.5 2.3 copy.36
  118.8 4.2 %all_gather.40 = bf16[2,2,256]{2,1,0:T(2,128)(2,1)S(1)} all-gather(bf16[1,2,256]{2,1,0:T(2,128)(2,1)S(1)} %all_gather.39), channel_id=1, replica_groups=mesh['seq_0'=8,'seq_1'=4,'seq_2'=2,'head'=4] {'seq_2'}, dimensions={0}, use_global_device_ids=true | all-gather | bytes 3072 | tf_op jit(solution)/shard_map/all_gather | solution.py:22
  123.0 6.7 %all_gather.41 = bf16[4,2,256]{2,1,0:T(2,128)(2,1)S(1)} all-gather(bf16[1,2,256]{2,1,0:T(2,128)(2,1)S(1)} %fusion.106), channel_id=1, replica_groups=mesh['seq_0'=8,'seq_1'=4,'seq_2'=2,'head'=4] {'seq_1'}, dimensions={0}, use_global_device_ids=true | all-gather | bytes 5120 | tf_op jit(solution)/shard_map/all_gather | solution.py:22
  129.7 14.9 %all_gather.42 = bf16[8,2,256]{2,1,0:T(2,128)(2,1)S(1)} all-gather(bf16[1,2,256]{2,1,0:T(2,128)(2,1)S(1)} %fusion.105), channel_id=1, replica_groups=mesh['seq_0'=8,'seq_1'=4,'seq_2'=2,'head'=4] {'seq_0'}, dimensions={0}, use_global_device_ids=true | all-gather | bytes 9216 | tf_op jit(solution)/shard_map/all_gather | solution.py:22
  144.6 2.8 %fusion.56 = f32[2,1,1024]{2,1,0:T(1,128)S(1)} fusion(bf16[1024,2,256]{2,0,1:T(8,128)(2,1)} %copy.36, f32[2,256,1]{1,0,2:T(2,128)S(1)} %fusion.94), kind=kOutput, calls=%fused_computation.76 | convolution fusion | flops 9437184 | bytes 1058816 | tf_op jit(solution)/shard_map/thd,hd->th/dot_general | solution.py:76
  147.4 8.4 %fusion.115 = (f32[2,1024]{1,0:T(2,128)S(1)}, f32[2,1024,1024]{1,2,0:T(8,128)}) fusion(pred[1024,1024]{0,1:T(8,128)(4,1)} %iota_compare_fusion, bf16[1024,2,256]{0,2,1:T(8,128)(2,1)} %bitcast.57, bf16[1024,2,256]{0,2,1:T(8,128)(2,1)} %bitcast.54), kind=kOutput, calls=%fused_computation.145 | convolution fusion | flops 1082131456 | bytes 11542528 | tf_op jit(solution)/shard_map/sub | solution.py:71
  155.8 6.3 %fusion.4 = f32[2,256,1024]{2,1,0:T(8,128)} fusion(bf16[1024,2,256]{0,2,1:T(8,128)(2,1)} %bitcast.59, f32[2,1024,1024]{1,2,0:T(8,128)} %get-tuple-element.8, f32[2,1024]{1,0:T(2,128)S(1)} %get-tuple-element.7), kind=kOutput, calls=%fused_computation.14 | convolution fusion | flops 1077936128 | bytes 11542528 | tf_op jit(solution)/shard_map/hqk,khd->qhd/dot_general | solution.py:73
  162.1 0.0 all-gather.10.cloned.1.call-done
  162.1 7.4 %fusion.15 = bf16[1024,2,256]{0,2,1:T(8,128)(2,1)} fusion(f32[2,256,1024]{2,1,0:T(8,128)} %fusion.4, f32[2]{0:T(128)S(1)} %get-tuple-element.5, f32[1024,2]{0,1:T(2,128)S(1)} %fusion.90, f32[2]{0:T(128)S(1)} %get-tuple-element.6, bf16[1024,2,256]{2,0,1:T(8,128)(2,1)} %copy.36, bf16[8,2,256,256]{3,2,1,0:T(8,128)(2,1)} %all-gather.10.cloned.1.call-done, ...), kind=kOutput, calls=%fused_computation.26 | convolution fusion | flops 1621753856 | bytes 7872542 | tf_op jit(solution)/shard_map/thd,hde->the/dot_general | solution.py:75
  169.5 0.0 all-gather.12.cloned.1.call-update
  169.5 4.0 %copy.41 = bf16[512,2048]{0,1:T(8,128)(2,1)} copy(bf16[512,2048]{1,0:T(8,128)(2,1)} %param.10) | data formatting | bytes 4194304 | tf_op args[4]
  173.5 39.7 %all_to_all.19 = bf16[512,4,512]{0,2,1:T(8,128)(2,1)} all-to-all(bf16[512,4,512]{0,2,1:T(8,128)(2,1)} %bitcast.51), channel_id=1, replica_groups=mesh['seq_0'=8,'seq_1'=4,'seq_2'=2,'head'=4] {'head'}, dimensions={1} | all-to-all | bytes 4194304 | tf_op jit(solution)/shard_map/all_to_all | solution.py:80
  213.2 4.2 %copy.42 = bf16[4,512,512]{2,1,0:T(8,128)(2,1)} copy(bf16[4,512,512]{1,2,0:T(8,128)(2,1)} %bitcast.50) | data formatting | bytes 4194304 | tf_op jit(solution)/shard_map/all_to_all | solution.py:80
  217.4 21.0 %all-gather.12.cloned.1.call-done = bf16[1024,2048]{0,1:T(8,128)(2,1)} async-done(((bf16[1024,512]{0,1:T(8,128)(2,1)}), bf16[1024,2048]{0,1:T(8,128)(2,1)}) %all-gather.12.cloned.1.call-update) | async-done | bytes 4194320 | tf_op jit(solution)/shard_map/all_gather | solution.py:82
  238.4 6.2 %convolution_convert_fusion = bf16[1024,512]{1,0:T(8,128)(2,1)} fusion(bf16[1024,2048]{0,1:T(8,128)(2,1)} %all-gather.12.cloned.1.call-done, bf16[2048,512]{1,0:T(8,128)(2,1)} %bitcast.52), kind=kOutput, calls=%fused_computation.29 | convolution fusion | flops 2148007936 | bytes 7340032 | tf_op jit(solution)/shard_map/dot_general | solution.py:81
  (6 shorter events, 0.1 us)
Async XLA Ops:
  6.5 57.0 %copy-start = (bf16[2048,512]{1,0:T(8,128)(2,1)S(1)}, bf16[2048,512]{1,0:T(8,128)(2,1)}, u32[]{:S(2)}) copy-start(bf16[2048,512]{1,0:T(8,128)(2,1)} %param.8) | copy-start | bytes 6291460
  6.5 57.0 %all-gather.6.cloned.1.call-start = ((), (), s32[]{:S(2)}) async-start(), calls=%async_computation.1 | async-start | bytes 5242880 | tf_op jit(solution)/shard_map/all_gather | solution.py:52
  7.3 99.6 %all-gather.8.cloned.1.call-start = ((), (), s32[]{:S(2)}) async-start(), calls=%async_computation.2 | async-start | bytes 1310720 | tf_op jit(solution)/shard_map/all_gather | solution.py:22
  72.1 5.3 %copy-start.1 = (bf16[1024,2,256]{2,0,1:T(8,128)(2,1)S(1)}, bf16[1024,2,256]{2,0,1:T(8,128)(2,1)}, u32[]{:S(2)}) copy-start(bf16[1024,2,256]{2,0,1:T(8,128)(2,1)} %copy.33) | copy-start | bytes 3145732
  77.4 1.3 copy-start.3
  77.4 4.8 %copy-start.2 = (f32[2]{0:T(128)S(1)}, f32[2]{0:T(128)}, u32[]{:S(2)}) copy-start(f32[2]{0:T(128)} %param.11) | copy-start | bytes 28
  82.1 80.0 %all-gather.10.cloned.1.call-start = ((), (), s32[]{:S(2)}) async-start(), calls=%async_computation.3 | async-start | bytes 2359296 | tf_op jit(solution)/shard_map/all_gather | solution.py:22
  108.9 129.4 %all-gather.12.cloned.1.call-start = ((), (), s32[]{:S(2)}) async-start(), calls=%async_computation.4 | async-start | bytes 5242880 | tf_op jit(solution)/shard_map/all_gather | solution.py:82
Sparse Core Ops, SparseCore 0:
  9.1 54.3 all-gather.5
  82.2 24.5 all-gather.7
  109.0 39.1 all-gather.9
  169.6 68.6 all-gather.11
where the time goes:
time: 252 us; the launch traced here: 251 us
  waiting for transfers between devices  103 us (41%)
  blocking collectives  68.1 us (27%)
  matrix products  50.1 us (20%)
  between operations  13.2 us (5%)
  local copies, waits for them, and re-layouts  12.8 us (5%)
  other arithmetic  4.18 us (2%)
    all_gather x1, waiting for transfers between devices, on_device(): piece = lax.all_gather(tokens, 'head', axis=1, tiled=True)  56.3 us
    all_to_all x1, blocking collectives, on_device(): lax.all_to_all(w_out, 'head', split_axis=1, concat_axis=0, tiled=True)  39.7 us
    all_gather x4, blocking collectives, carried_in(): lax.all_gather(part.astype(kind), axis)  28.4 us
    all_gather x2, waiting for transfers between devices, carried_in(): lax.all_gather(part.astype(kind), axis)  24.7 us
    all_gather x1, waiting for transfers between devices, on_device(): lax.all_gather(mixed, 'head', axis=1, tiled=True)  21 us
    dot_general x3, matrix products, on_device(): result.append(jnp.dot(piece, weight, preferred_element_type=jnp.float32))  17.7 us
    sub x1, matrix products, on_device(): expo = jnp.exp(scores - jnp.max(scores, axis=2, keepdims=True))  8.38 us
    dot_general x1, matrix products, on_device(): jnp.einsum('thd,hde->the', fquery, memory, precision=lax.Precision.HIGHEST)  7.36 us
  transfers between devices with their start and end apart: 4, of which 3 were waited for; matrix products, arithmetic and copies ran while one was open for 14% of the time, Pallas kernels for 0%

commit v1 on v0

--- a/solution.py
+++ b/solution.py
@@ -1,3 +1,4 @@
+import functools
 import jax
 import jax.numpy as jnp
 from jax import lax
@@ -5,6 +6,14 @@
 from jax.sharding import PartitionSpec as P
 
 SEQ = ("seq_0", "seq_1", "seq_2")
+
+
+def extend_group(state, bus_axis):
+    s_next = jnp.concatenate([state] * lax.axis_size(bus_axis), axis=1)
+    return lax.all_to_all(s_next, bus_axis, split_axis=1, tiled=True, concat_axis=1)
+
+
+apply_the_sites = functools.partial(extend_group, bus_axis="head")
 
 
 def nothing_yet(shard, identity):
@@ -78,11 +87,7 @@
     share = jax.nn.sigmoid(mix_logit)[None, :, None]
     mixed = (share * readout + (1.0 - share) * local).astype(jnp.bfloat16).reshape(seg, width)
     columns = lax.all_to_all(w_out, "head", split_axis=1, concat_axis=0, tiled=True)
-    summed = jnp.dot(
-        lax.all_gather(mixed, "head", axis=1, tiled=True),
-        columns,
-        preferred_element_type=jnp.float32,
-    )
+    summed = jnp.dot(apply_the_sites(mixed), columns, preferred_element_type=jnp.float32)
     return summed.astype(jnp.bfloat16)
 
 

time: 252 us -> 232 us (0.921)
  waiting for transfers between devices: 103 us -> 69.3 us
  blocking collectives: 68.1 us -> 76.3 us
  starting transfers between devices: 0.13 us -> 4.68 us
    all_gather x1 -> x0, waiting for transfers between devices: 21 us -> none  [on_device(): lax.all_gather(mixed, 'head', axis=1, tiled=True)]
    all_gather x2, waiting for transfers between devices: 24.7 us -> 12.2 us  [carried_in(): lax.all_gather(part.astype(kind), axis)]
    all_to_all x1, blocking collectives: 39.7 us -> 48.1 us  [extend_group(): lax.all_to_all(s_next, bus_axis, split_axis=1, tiled=True, concat_axis=1)]
    all_to_all x0 -> x1, starting transfers between devices: none -> 4.6 us  [on_device(): lax.all_to_all(w_out, 'head', split_axis=1, concat_axis=0, tiled=True)]
  transfers between devices with their start and end apart: 4 -> 4, of which waited for: 3 -> 2; matrix products, arithmetic and copies ran while one was open for 14% -> 20% of each run, Pallas kernels for 0% -> 0%
where the time goes in v1:
time: 232 us; the launch traced here: 229 us
  blocking collectives  76.3 us (33%)
  waiting for transfers between devices  69.3 us (30%)
  matrix products  47.8 us (21%)
  local copies, waits for them, and re-layouts  13.5 us (6%)
  between operations  13.2 us (6%)
  starting transfers between devices  4.68 us (2%)
  other arithmetic  4.14 us (2%)
    all_gather x1, waiting for transfers between devices, on_device(): piece = lax.all_gather(tokens, 'head', axis=1, tiled=True)  56.3 us
    all_to_all x1, blocking collectives, extend_group(): lax.all_to_all(s_next, bus_axis, split_axis=1, tiled=True, concat_axis=1)  48.1 us
    all_gather x4, blocking collectives, carried_in(): lax.all_gather(part.astype(kind), axis)  28.1 us
    dot_general x3, matrix products, on_device(): result.append(jnp.dot(piece, weight, preferred_element_type=jnp.float32))  16.9 us
    all_gather x2, waiting for transfers between devices, carried_in(): lax.all_gather(part.astype(kind), axis)  12.2 us
    sub x1, matrix products, on_device(): expo = jnp.exp(scores - jnp.max(scores, axis=2, keepdims=True))  8.37 us
    dot_general x1, matrix products, on_device(): jnp.einsum('thd,hde->the', fquery, memory, precision=lax.Precision.HIGHEST)  7.37 us
    dot_general x1, matrix products, on_device(): jnp.einsum('hqk,khd->qhd', probs, values, preferred_element_type=jnp.floa...  6.28 us
  transfers between devices with their start and end apart: 4, of which 2 were waited for; matrix products, arithmetic and copies ran while one was open for 20% of the time, Pallas kernels for 0%

profile of v1, /device:TPU:1, one launch (start us, length us, event | category | flops | bytes accessed | tf_op | source)
XLA Modules:
  0.0 229.0 jit_solution(29620586906321145)
XLA Ops:
  6.5 0.0 copy-start
  6.5 0.0 all-gather.5.cloned.1.call-start
  6.5 0.7 all-gather.5.cloned.1.call-update
  7.3 0.0 all-gather.7.cloned.1.call-start
  7.3 56.3 %all-gather.5.cloned.1.call-done = bf16[1024,2048]{1,0:T(8,128)(2,1)} async-done(((bf16[1024,512]{1,0:T(8,128)(2,1)}), bf16[1024,2048]{1,0:T(8,128)(2,1)}) %all-gather.5.cloned.1.call-update) | async-done | bytes 4194320 | tf_op jit(solution)/shard_map/all_gather | solution.py:61
  63.6 0.0 copy-done
  63.6 5.3 %fusion.24 = (bf16[512]{0:T(512)(128)(2,1)S(1)}, bf16[1024,512]{0,1:T(8,128)(2,1)S(1)}) fusion(bf16[1024,2048]{1,0:T(8,128)(2,1)} %all-gather.5.cloned.1.call-done, bf16[2048,512]{1,0:T(8,128)(2,1)S(1)} %copy-done), kind=kOutput, calls=%fused_computation.38 | convolution fusion | flops 2151677440 | bytes 7341056 | tf_op jit(solution)/shard_map/dot_general | solution.py:64
  68.9 0.0 copy-start.1
  68.9 1.3 copy.27
  70.2 0.0 copy-start.2
  70.2 5.3 %convolution_convert_fusion.1 = bf16[1024,512]{0,1:T(8,128)(2,1)S(1)} fusion(bf16[1024,2048]{1,0:T(8,128)(2,1)} %all-gather.5.cloned.1.call-done, bf16[2048,512]{1,0:T(8,128)(2,1)} %param.9), kind=kOutput, calls=%fused_computation.33 | convolution fusion | flops 2148007936 | bytes 7340032 | tf_op jit(solution)/shard_map/dot_general | solution.py:64
  75.5 0.0 copy-done.1
  75.5 0.0 copy-start.4
  75.6 0.0 copy-done.2
  75.6 1.2 convolution_convert_fusion.3
  76.8 0.0 copy-done.4
  76.8 2.6 %all-gather = bf16[4,256,256]{2,1,0:T(8,128)(2,1)S(1)} all-gather(bf16[2,256,256]{2,1,0:T(8,128)(2,1)S(1)} %convolution_convert_fusion.3), channel_id=2, replica_groups=mesh['seq_0'=8,'seq_1'=4,'seq_2'=2,'head'=4] {'seq_2'}, dimensions={0}, use_global_device_ids=true | all-gather | bytes 786432 | tf_op jit(solution)/shard_map/all_gather | solution.py:31
  79.5 0.8 fusion.63
  80.3 0.0 all-gather.7.cloned.1.call-update
  80.3 3.9 %copy.36 = bf16[512,2048]{0,1:T(8,128)(2,1)} copy(bf16[512,2048]{1,0:T(8,128)(2,1)} %param.10) | data formatting | bytes 4194304 | tf_op args[4]
  84.2 4.2 %copy.37 = bf16[512,4,512]{2,0,1:T(8,128)(2,1)} copy(bf16[512,4,512]{0,2,1:T(8,128)(2,1)} %bitcast.54) | data formatting | bytes 4194304 | tf_op jit(solution)/shard_map/all_to_all | solution.py:89
  88.4 0.0 copy-start.3
  88.4 4.6 %all-to-all-start.1 = ((bf16[512,4,512]{2,0,1:T(8,128)(2,1)}), bf16[512,4,512]{2,0,1:T(8,128)(2,1)}, u32[]{:S(2)}, u32[]{:S(2)}) async-start(bf16[512,4,512]{2,0,1:T(8,128)(2,1)} %copy.37), calls=%async_computation.1 | async-start | bytes 4194304 | tf_op jit(solution)/shard_map/all_to_all | solution.py:89
  93.0 0.0 all-gather.9.cloned.1.call-start
  93.1 0.0 copy-done.3
  93.1 12.2 %all-gather.7.cloned.1.call-done = bf16[4,2,256,256]{3,2,1,0:T(8,128)(2,1)} async-done(((bf16[1,2,256,256]{3,2,1,0:T(8,128)(2,1)}), bf16[4,2,256,256]{3,2,1,0:T(8,128)(2,1)}) %all-gather.7.cloned.1.call-update) | async-done | bytes 1048592 | tf_op jit(solution)/shard_map/all_gather | solution.py:31
  105.3 2.0 fusion.59
  107.3 0.0 all-gather.9.cloned.1.call-update
  107.4 1.3 iota_compare_fusion
  108.6 6.2 %convolution_convert_fusion = bf16[1024,512]{0,1:T(8,128)(2,1)} fusion(bf16[1024,2048]{1,0:T(8,128)(2,1)} %all-gather.5.cloned.1.call-done, bf16[2048,512]{1,0:T(8,128)(2,1)} %param.7), kind=kOutput, calls=%fused_computation.32 | convolution fusion | flops 2148007936 | bytes 7340032 | tf_op jit(solution)/shard_map/dot_general | solution.py:64
  114.9 2.3 copy.30
  117.2 3.9 %all_gather.37 = bf16[2,2,256]{2,1,0:T(2,128)(2,1)S(1)} all-gather(bf16[1,2,256]{2,1,0:T(2,128)(2,1)S(1)} %all_gather.36), channel_id=1, replica_groups=mesh['seq_0'=8,'seq_1'=4,'seq_2'=2,'head'=4] {'seq_2'}, dimensions={0}, use_global_device_ids=true | all-gather | bytes 3072 | tf_op jit(solution)/shard_map/all_gather | solution.py:31
  121.1 6.5 %all_gather.38 = bf16[4,2,256]{2,1,0:T(2,128)(2,1)S(1)} all-gather(bf16[1,2,256]{2,1,0:T(2,128)(2,1)S(1)} %fusion.110), channel_id=1, replica_groups=mesh['seq_0'=8,'seq_1'=4,'seq_2'=2,'head'=4] {'seq_1'}, dimensions={0}, use_global_device_ids=true | all-gather | bytes 5120 | tf_op jit(solution)/shard_map/all_gather | solution.py:31
  127.6 15.1 %all_gather.39 = bf16[8,2,256]{2,1,0:T(2,128)(2,1)S(1)} all-gather(bf16[1,2,256]{2,1,0:T(2,128)(2,1)S(1)} %fusion.109), channel_id=1, replica_groups=mesh['seq_0'=8,'seq_1'=4,'seq_2'=2,'head'=4] {'seq_0'}, dimensions={0}, use_global_device_ids=true | all-gather | bytes 9216 | tf_op jit(solution)/shard_map/all_gather | solution.py:31
  142.7 2.8 %fusion.60 = f32[2,1,1024]{2,1,0:T(1,128)S(1)} fusion(bf16[1024,2,256]{2,0,1:T(8,128)(2,1)} %copy.30, f32[2,256,1]{1,0,2:T(2,128)S(1)} %fusion.98), kind=kOutput, calls=%fused_computation.78 | convolution fusion | flops 9437184 | bytes 1058816 | tf_op jit(solution)/shard_map/thd,hd->th/dot_general | solution.py:85
  145.5 8.4 %fusion.119 = (f32[2,1024]{1,0:T(2,128)S(1)}, f32[2,1024,1024]{1,2,0:T(8,128)}) fusion(pred[1024,1024]{0,1:T(8,128)(4,1)} %iota_compare_fusion, bf16[1024,2,256]{0,2,1:T(8,128)(2,1)} %bitcast.58, bf16[1024,2,256]{0,2,1:T(8,128)(2,1)} %bitcast.56), kind=kOutput, calls=%fused_computation.147 | convolution fusion | flops 1082131456 | bytes 11542528 | tf_op jit(solution)/shard_map/sub | solution.py:80
  153.9 6.3 %fusion.4 = f32[2,256,1024]{2,1,0:T(8,128)} fusion(bf16[1024,2,256]{0,2,1:T(8,128)(2,1)} %bitcast.61, f32[2,1024,1024]{1,2,0:T(8,128)} %get-tuple-element.8, f32[2,1024]{1,0:T(2,128)S(1)} %get-tuple-element.7), kind=kOutput, calls=%fused_computation.14 | convolution fusion | flops 1077936128 | bytes 11542528 | tf_op jit(solution)/shard_map/hqk,khd->qhd/dot_general | solution.py:82
  160.2 0.0 all-gather.9.cloned.1.call-done
  160.2 7.4 %fusion.17 = bf16[1024,2,256]{0,2,1:T(8,128)(2,1)} fusion(f32[2,256,1024]{2,1,0:T(8,128)} %fusion.4, f32[2]{0:T(128)S(1)} %get-tuple-element.5, f32[1024,2]{0,1:T(2,128)S(1)} %fusion.94, f32[2]{0:T(128)S(1)} %get-tuple-element.6, bf16[1024,2,256]{2,0,1:T(8,128)(2,1)} %copy.30, bf16[8,2,256,256]{3,2,1,0:T(8,128)(2,1)} %all-gather.9.cloned.1.call-done, ...), kind=kOutput, calls=%fused_computation.29 | convolution fusion | flops 1621753856 | bytes 7872542 | tf_op jit(solution)/shard_map/thd,hde->the/dot_general | solution.py:84
  167.6 1.5 copy.35
  169.1 0.0 all-to-all-done.1
  169.1 0.3 concatenate.7
  169.4 48.1 %all_to_all.22 = bf16[1024,4,512]{2,0,1:T(8,128)(2,1)S(1)} all-to-all(bf16[1024,4,512]{2,0,1:T(8,128)(2,1)S(1)} %concatenate.7), channel_id=1, replica_groups=mesh['seq_0'=8,'seq_1'=4,'seq_2'=2,'head'=4] {'head'}, dimensions={1} | all-to-all | bytes 8388608 | tf_op jit(solution)/shard_map/all_to_all | solution.py:13
  217.5 4.9 %bitcast_convert_fusion = bf16[1024,512]{1,0:T(8,128)(2,1)} fusion(bf16[1024,4,512]{2,0,1:T(8,128)(2,1)S(1)} %all_to_all.22, bf16[512,4,512]{2,0,1:T(8,128)(2,1)} %all-to-all-done.1), kind=kOutput, calls=%fused_computation.25 | convolution fusion | flops 2148007936 | bytes 7340032 | tf_op jit(solution)/shard_map/dot_general | solution.py:90
  (6 shorter events, 0.1 us)
Async XLA Ops:
  6.5 57.0 %copy-start = (bf16[2048,512]{1,0:T(8,128)(2,1)S(1)}, bf16[2048,512]{1,0:T(8,128)(2,1)}, u32[]{:S(2)}) copy-start(bf16[2048,512]{1,0:T(8,128)(2,1)} %param.8) | copy-start | bytes 6291460
  6.5 57.0 %all-gather.5.cloned.1.call-start = ((), (), s32[]{:S(2)}) async-start(), calls=%async_computation.2 | async-start | bytes 5242880 | tf_op jit(solution)/shard_map/all_gather | solution.py:61
  7.3 98.1 %all-gather.7.cloned.1.call-start = ((), (), s32[]{:S(2)}) async-start(), calls=%async_computation.3 | async-start | bytes 1310720 | tf_op jit(solution)/shard_map/all_gather | solution.py:31
  68.9 6.6 %copy-start.1 = (bf16[1024,512]{0,1:T(8,128)(2,1)}, bf16[1024,512]{0,1:T(8,128)(2,1)S(1)}, u32[]{:S(2)}) copy-start(bf16[1024,512]{0,1:T(8,128)(2,1)S(1)} %get-tuple-element.10) | copy-start | bytes 3145732
  70.2 5.3 %copy-start.2 = (bf16[1024,2,256]{2,0,1:T(8,128)(2,1)S(1)}, bf16[1024,2,256]{2,0,1:T(8,128)(2,1)}, u32[]{:S(2)}) copy-start(bf16[1024,2,256]{2,0,1:T(8,128)(2,1)} %copy.27) | copy-start | bytes 3145732
  75.5 1.3 copy-start.4
  88.4 4.7 %copy-start.3 = (f32[2]{0:T(128)S(1)}, f32[2]{0:T(128)}, u32[]{:S(2)}) copy-start(f32[2]{0:T(128)} %param.11) | copy-start | bytes 28
  88.4 80.7 %all-to-all-start.1 = ((bf16[512,4,512]{2,0,1:T(8,128)(2,1)}), bf16[512,4,512]{2,0,1:T(8,128)(2,1)}, u32[]{:S(2)}, u32[]{:S(2)}) async-start(bf16[512,4,512]{2,0,1:T(8,128)(2,1)} %copy.37), calls=%async_computation.1 | async-start | bytes 4194304 | tf_op jit(solution)/shard_map/all_to_all | solution.py:89
  93.0 67.2 %all-gather.9.cloned.1.call-start = ((), (), s32[]{:S(2)}) async-start(), calls=%async_computation.4 | async-start | bytes 2359296 | tf_op jit(solution)/shard_map/all_gather | solution.py:31
Sparse Core Ops, SparseCore 0:
  9.1 54.3 all-gather.4
  80.4 24.8 all-gather.6
  107.5 38.8 all-gather.8
